TPU v7x, 128 devices: a whole 4x4x4 slice. The times are simulated.
128 devices in a mesh: dp: 1, sp: 128 (over z, y, x, core).
Axes of the slice: x: 4, y: 4, z: 4, core: 2. Of those that a mesh axis runs over, the one named last changes fastest.
Arguments:
- patches: bfloat16 [4, 65536, 1024], P('dp', 'sp')
- ln1_scale: float32 [1024], replicated
- ln1_bias: float32 [1024], replicated
- w_tok1: bfloat16 [65536, 512], replicated
- b_tok1: float32 [512], replicated
- w_tok2: bfloat16 [512, 65536], replicated
- b_tok2: float32 [65536], replicated
- ln2_scale: float32 [1024], replicated
- ln2_bias: float32 [1024], replicated
- w_ch1: bfloat16 [1024, 4096], replicated
- b_ch1: float32 [4096], replicated
- w_ch2: bfloat16 [4096, 1024], replicated
- b_ch2: float32 [1024], replicated
Outputs:
- output: bfloat16 [4, 65536, 1024], P('dp', 'sp')
All inputs are finite; a program needn't handle non-finite values.
Results may differ from a plain program's by a relative error of at most 0.0111779.
Values are sent between devices in bfloat16 or wider.
A program may use at most 1 GiB of HBM per device.

v0:
```python
import jax
import jax.numpy as jnp
from jax import lax
from jax.sharding import PartitionSpec as P

LN_EPS = 1e-6


def layer_norm(rows, scale, offset):
    rows_wide = rows.astype(jnp.float32)
    row_mean = jnp.mean(rows_wide, axis=-1, keepdims=True)
    centered = rows_wide - row_mean
    row_var = jnp.mean(centered * centered, axis=-1, keepdims=True)
    return (centered * lax.rsqrt(row_var + LN_EPS) * scale + offset).astype(jnp.bfloat16)


def channel_mixing(residual, ln2_scale, ln2_bias, w_ch1, b_ch1, w_ch2, b_ch2):
    chan_in = layer_norm(residual, ln2_scale, ln2_bias)
    pre_act = jnp.einsum('bsc,ce->bse', chan_in, w_ch1, preferred_element_type=jnp.float32) + b_ch1
    act_ch = jax.nn.gelu(pre_act, approximate=True).astype(jnp.bfloat16)
    ch_out = jnp.einsum('bse,ec->bsc', act_ch, w_ch2, preferred_element_type=jnp.float32) + b_ch2
    return (residual.astype(jnp.float32) + ch_out).astype(jnp.bfloat16)


def solution(mesh):
    row_spec = P('dp', 'sp', None)
    full_spec = P()

    def local_layer(patches, ln1_scale, ln1_bias, w_tok1, b_tok1, w_tok2, b_tok2, ln2_scale, ln2_bias, w_ch1, b_ch1, w_ch2, b_ch2):
        normed = layer_norm(patches, ln1_scale, ln1_bias)
        normed_cols = lax.all_to_all(normed, 'sp', 2, 1, tiled=True)
        hidden = jnp.einsum('sd,bsc->bdc', w_tok1, normed_cols, preferred_element_type=jnp.float32)
        act_tok = jax.nn.gelu(hidden + b_tok1[None, :, None], approximate=True).astype(jnp.bfloat16)
        mixed = jnp.einsum('ds,bdc->bsc', w_tok2, act_tok, preferred_element_type=jnp.float32)
        mixed_cols = (mixed + b_tok2[None, :, None]).astype(jnp.bfloat16)
        mixed_rows = lax.all_to_all(mixed_cols, 'sp', 1, 2, tiled=True)
        residual = (patches.astype(jnp.float32) + mixed_rows.astype(jnp.float32)).astype(jnp.bfloat16)
        return channel_mixing(residual, ln2_scale, ln2_bias, w_ch1, b_ch1, w_ch2, b_ch2)

    return jax.shard_map(local_layer, mesh=mesh, in_specs=(row_spec,) + (full_spec,) * 12, out_specs=row_spec, check_vma=False)
```

profile of v0, /device:TPU:5, one launch (start us, length us, event | category | flops | bytes accessed | tf_op | source)
XLA Modules:
  0.0 588.9 jit_solution(8481046318947759585)
XLA Ops:
  0.0 3.0 convert_reduce_fusion.1
  3.0 3.0 fusion.23
  6.0 0.0 copy-done
  6.0 0.0 copy-done.2
  6.0 0.0 copy-done.3
  6.0 3.0 fusion.26
  9.0 7.8 %copy.22 = bf16[4,512,1024]{1,0,2:T(4,128)(2,1)} copy(bf16[4,512,1024]{2,1,0:T(8,128)(2,1)} %fusion.26) | data formatting | bytes 8388608 | tf_op jit(solution)/shard_map/convert_element_type | solution.py:14
  16.9 67.7 %all_to_all.27 = bf16[4,512,1024]{1,0,2:T(4,128)(2,1)S(1)} all-to-all(bf16[4,512,1024]{1,0,2:T(4,128)(2,1)} %copy.22), channel_id=1, replica_groups=mesh['dp'=1,'sp'=128] {'sp'}, dimensions={2} | all-to-all | bytes 8388608 | tf_op jit(solution)/shard_map/all_to_all | solution.py:31
  84.5 2.8 copy.23
  87.4 0.0 copy-done.4
  87.4 25.4 %fusion.67 = bf16[4,512,8]{1,2,0:T(8,128)(2,1)S(1)} fusion(bf16[4,65536,8]{1,2,0:T(8,128)(2,1)} %bitcast.53, bf16[65536,512]{1,0:T(8,128)(2,1)} %param.16, f32[512]{0:T(512)S(1)} %copy-done.4), kind=kOutput, calls=%fused_computation.54 | convolution fusion | flops 2147647488 | bytes 71337984 | tf_op jit(solution)/shard_map/sd,bsc->bdc/dot_general | solution.py:32
  112.8 0.0 copy-done.1
  112.8 26.2 %fusion.1 = bf16[4,65536,8]{1,2,0:T(8,128)(2,1)} fusion(bf16[4,512,8]{1,2,0:T(8,128)(2,1)S(1)} %fusion.67, bf16[512,65536]{1,0:T(8,128)(2,1)} %param.18, f32[65536]{0:T(1024)S(1)} %copy-done.1), kind=kOutput, calls=%fused_computation.2 | convolution fusion | flops 2151677952 | bytes 71598080 | tf_op jit(solution)/shard_map/ds,bdc->bsc/dot_general | solution.py:34
  139.0 68.3 %copy.24 = bf16[4,65536,8]{2,0,1:T(4,128)(2,1)} copy(bf16[4,65536,8]{1,2,0:T(8,128)(2,1)} %fusion.1) | data formatting | bytes 8388608 | tf_op jit(solution)/shard_map/convert_element_type | solution.py:35
  207.3 77.4 %reshape.42 = bf16[128,2,8192]{2,1,0:T(2,128)(2,1)} reshape(bf16[65536,4,8]{2,1,0:T(4,128)(2,1)} %bitcast.44) | data formatting | bytes 8388608
  284.7 73.6 %all_to_all.28 = bf16[128,2,8192]{2,1,0:T(2,128)(2,1)} all-to-all(bf16[128,2,8192]{2,1,0:T(2,128)(2,1)} %reshape.42), channel_id=1, replica_groups=mesh['dp'=1,'sp'=128] {'sp'}, dimensions={0} | all-to-all | bytes 8388608 | tf_op jit(solution)/shard_map/all_to_all | solution.py:36
  358.3 80.3 %reshape.43 = bf16[65536,4,8]{2,1,0:T(4,128)(2,1)} reshape(bf16[128,2,8192]{2,1,0:T(2,128)(2,1)} %all_to_all.28) | data formatting | bytes 8388608
  438.6 75.0 %copy.25 = bf16[4,65536,8]{1,2,0:T(8,128)(2,1)} copy(bf16[4,65536,8]{2,0,1:T(4,128)(2,1)} %bitcast.45) | data formatting | bytes 8388608 | tf_op jit(solution)/shard_map/all_to_all | solution.py:36
  513.5 6.6 %convert_bitcast_fusion = f32[4,512,1024]{1,2,0:T(8,128)} fusion(bf16[4,128,512,8]{2,3,1,0:T(8,128)(2,1)} %bitcast.54), kind=kLoop, calls=%fused_computation.36 | loop fusion | flops 2097152 | bytes 12582912 | tf_op jit(solution)/shard_map/convert_element_type | solution.py:37
  520.1 8.7 %copy.26 = f32[4,512,1024]{2,1,0:T(8,128)} copy(f32[4,512,1024]{1,2,0:T(8,128)} %convert_bitcast_fusion) | data formatting | bytes 16777216 | tf_op jit(solution)/shard_map/convert_element_type | solution.py:37
  528.9 5.8 convert_reduce_fusion
  534.6 1.4 fusion.19
  536.1 0.0 copy-done.5
  536.1 0.0 copy-done.6
  536.1 0.0 copy-done.7
  536.1 0.0 slice-start.1
  536.1 0.0 copy-start.8
  536.1 31.3 %fusion.86 = bf16[4,512,4096]{2,1,0:T(8,128)(2,1)} fusion(f32[4096]{0:T(1024)S(1)} %copy-done.5, bf16[1024,4096]{1,0:T(8,128)(2,1)} %param.22, bf16[4,512,1024]{2,1,0:T(8,128)(2,1)S(1)} %get-tuple-element.6, f32[1024]{0:T(1024)S(1)} %copy-done.6, f32[1024]{0:T(1024)S(1)} %copy-done.7, f32[4,512]{1,0:T(4,128)S(1)} %add_rsqrt_fusion, ...), kind=kOutput, calls=%fused_computation.14.clone.clone.clone.clone.1 | convolution fusion | flops 17276338176 | bytes 29401088 | tf_op jit(solution)/shard_map/bsc,ce->bse/dot_general | solution.py:19
  567.4 0.0 slice-done
  567.4 0.0 slice-done.1
  567.4 0.0 copy-done.8
  567.4 21.4 %fusion.28 = bf16[4,512,1024]{2,1,0:T(8,128)(2,1)} fusion(bf16[4,512,1024]{2,1,0:T(8,128)(2,1)S(1)} %get-tuple-element.6, f32[1024]{0:T(1024)S(1)} %copy-done.8, bf16[4096,1024]{1,0:T(8,128)(2,1)S(1)} %bitcast.56, bf16[4,512,4096]{2,1,0:T(8,128)(2,1)} %fusion.86), kind=kOutput, calls=%fused_computation.35 | convolution fusion | flops 17188257792 | bytes 33558528 | tf_op jit(solution)/shard_map/bse,ec->bsc/dot_general | solution.py:21
  (14 shorter events, 0.0 us)
Async XLA Ops:
  0.0 6.0 %copy-start = (bf16[4,512,1024]{2,1,0:T(8,128)(2,1)S(1)}, bf16[4,512,1024]{2,1,0:T(8,128)(2,1)}, u32[]{:S(2)}) copy-start(bf16[4,512,1024]{2,1,0:T(8,128)(2,1)} %param.13) | copy-start | bytes 12582916
  0.0 6.0 %copy-start.2 = (f32[1024]{0:T(1024)S(1)}, f32[1024]{0:T(1024)}, u32[]{:S(2)}) copy-start(f32[1024]{0:T(1024)} %param.15) | copy-start | bytes 12292
  0.0 6.0 %copy-start.3 = (f32[1024]{0:T(1024)S(1)}, f32[1024]{0:T(1024)}, u32[]{:S(2)}) copy-start(f32[1024]{0:T(1024)} %param.14) | copy-start | bytes 12292
  16.9 70.5 %copy-start.4 = (f32[512]{0:T(512)S(1)}, f32[512]{0:T(512)}, u32[]{:S(2)}) copy-start(f32[512]{0:T(512)} %param.17) | copy-start | bytes 6148
  87.4 25.4 %copy-start.1 = (f32[65536]{0:T(1024)S(1)}, f32[65536]{0:T(1024)}, u32[]{:S(2)}) copy-start(f32[65536]{0:T(1024)} %param.19) | copy-start | bytes 786436
  528.9 7.2 %copy-start.5 = (f32[4096]{0:T(1024)S(1)}, f32[4096]{0:T(1024)}, u32[]{:S(2)}) copy-start(f32[4096]{0:T(1024)} %param.23) | copy-start | bytes 49156
  528.9 7.2 %copy-start.6 = (f32[1024]{0:T(1024)S(1)}, f32[1024]{0:T(1024)}, u32[]{:S(2)}) copy-start(f32[1024]{0:T(1024)} %param.21) | copy-start | bytes 12292
  528.9 7.2 %copy-start.7 = (f32[1024]{0:T(1024)S(1)}, f32[1024]{0:T(1024)}, u32[]{:S(2)}) copy-start(f32[1024]{0:T(1024)} %param.20) | copy-start | bytes 12292
  528.9 38.6 %slice-start = ((s8[8388608]{0:T(1024)(128)(4,1)}), s8[4194304]{0:T(1024)(128)(4,1)S(1)}, s32[]{:S(2)}) async-start(s8[8388608]{0:T(1024)(128)(4,1)} %bitcast.55), calls=%async_computation.2 | async-start | bytes 8388608
  536.1 31.3 %slice-start.1 = ((s8[8388608]{0:T(1024)(128)(4,1)}), s8[4194304]{0:T(1024)(128)(4,1)S(1)}, s32[]{:S(2)}) async-start(s8[8388608]{0:T(1024)(128)(4,1)} %bitcast.55), calls=%async_computation.3 | async-start | bytes 8388608
  536.1 31.3 %copy-start.8 = (f32[1024]{0:T(1024)S(1)}, f32[1024]{0:T(1024)}, u32[]{:S(2)}) copy-start(f32[1024]{0:T(1024)} %param.25) | copy-start | bytes 12292
where the time goes:
time: 600 us; the launch traced here: 589 us
  local copies, waits for them, and re-layouts  320 us (53%)
  blocking collectives  141 us (24%)
  matrix products  104 us (17%)
  other arithmetic  22.7 us (4%)
    unnamed x24, local copies, waits for them, and re-layouts  158 us
    all_to_all x1, local copies, waits for them, and re-layouts, local_layer(): mixed_rows = lax.all_to_all(mixed_cols, 'sp', 1, 2, tiled=True)  75 us
    all_to_all x1, blocking collectives, local_layer(): mixed_rows = lax.all_to_all(mixed_cols, 'sp', 1, 2, tiled=True)  73.6 us
    convert_element_type x1, local copies, waits for them, and re-layouts, local_layer(): mixed_cols = (mixed + b_tok2[None, :, None]).astype(jnp.bfloat16)  68.3 us
    all_to_all x1, blocking collectives, local_layer(): normed_cols = lax.all_to_all(normed, 'sp', 2, 1, tiled=True)  67.7 us
    dot_general x1, matrix products, channel_mixing(): jnp.einsum('bsc,ce->bse', chan_in, w_ch1, preferred_element_type=jnp.floa...  31.3 us
    dot_general x1, matrix products, local_layer(): jnp.einsum('ds,bdc->bsc', w_tok2, act_tok, preferred_element_type=jnp.flo...  26.2 us
    dot_general x1, matrix products, local_layer(): jnp.einsum('sd,bsc->bdc', w_tok1, normed_cols, preferred_element_type=jnp...  25.4 us

commit v1 on v0

v1 whole, which is shorter than its diff:
```python
import functools
import math

import jax
import jax.numpy as jnp
from jax import lax
from jax.experimental import pallas as pl
from jax.experimental.pallas import tpu as pltpu
from jax.sharding import PartitionSpec as P

LN_EPS = 1e-6
IMAGES = 4
ROWS = 512
CH = 1024
TOK = 512
HID = 4096
RING = 4
LANES = 128
UNITS = CH // 2 // LANES
BLOCK = (128, 32, 8)
E_TILE = 512
N_SLOTS = HID // E_TILE
F32 = jnp.float32
BF16 = jnp.bfloat16

GELU_A = math.sqrt(2.0 / math.pi)
GELU_B = GELU_A * 0.044715


def gelu(a):
    return (0.5 * a) * (1.0 + jnp.tanh(a * (GELU_A + GELU_B * (a * a))))


def layer_norm(rows, scale, offset):
    wide = rows.astype(F32)
    mean = jnp.mean(wide, axis=-1, keepdims=True)
    centered = wide - mean
    var = jnp.mean(centered * centered, axis=-1, keepdims=True)
    return (centered * lax.rsqrt(var + LN_EPS) * scale + offset).astype(BF16)


def layer_kernel(
    x_hbm, w_tok1_hbm, w_tok2_hbm, w_ch1_hbm, w_ch2_hbm,
    ln1_s, ln1_b, b_tok1, b_tok2, ln2_s, ln2_b, b_ch1, b_ch2,
    out_hbm,
    xv, w1raw, w2raw, w1t, w2t, wc1, wc2, b1col, b2col,
    usend, upair, part, got0, got1, got2, sum1, sum2, g, v, acc,
    load_sem, store_sem, u_send, u_recv, rs_send, rs_recv, ag_send, ag_recv, d_send, d_recv,
):
    me = lax.axis_index('sp')
    core = me % 2
    chip = me // 2
    partner = chip * 2 + (1 - core)

    def at(index):
        return {'sp': index}

    def geometry(b, q):
        color = (q + core + b) % 3
        places, strides = [], []
        for p in range(3):
            axis = (color + p) % 3
            stride = 1 + (3 * axis * (3 * axis - 1)) // 2
            strides.append(stride)
            places.append((chip // stride) % RING)
        return places, strides

    def peer(place, stride, j):
        other = (place + j) % RING
        return other, (chip + (other - place) * stride) * 2 + core

    loads = []

    def load(n, src, dst):
        c = pltpu.make_async_copy(src, dst, load_sem.at[n])
        c.start()
        loads.append(c)

    load(0, x_hbm.at[0], xv.at[0])
    load(1, w_tok1_hbm.at[pl.ds(pl.multiple_of(chip * (2 * ROWS), 2 * ROWS), 2 * ROWS)], w1raw)
    for b in range(1, IMAGES):
        load(1 + b, x_hbm.at[b], xv.at[b])
    load(5, w_tok2_hbm.at[:, pl.ds(pl.multiple_of(me * ROWS, ROWS), ROWS)], w2raw)
    load(6, w_ch1_hbm, wc1)
    load(7, w_ch2_hbm, wc2)

    barrier = pltpu.get_barrier_semaphore()
    pl.semaphore_signal(barrier, inc=1, device_id=at(partner), device_id_type=pl.DeviceIdType.MESH)
    for stride in (1, 4, 16):
        place = (chip // stride) % RING
        for j in range(1, RING):
            _, other = peer(place, stride, j)
            pl.semaphore_signal(barrier, inc=1, device_id=at(other), device_id_type=pl.DeviceIdType.MESH)

    def remote(src, dst, send, recv, device):
        return pltpu.make_async_remote_copy(
            src_ref=src, dst_ref=dst, send_sem=send, recv_sem=recv,
            device_id=at(device), device_id_type=pl.DeviceIdType.MESH)

    def arrived(ref, sem):
        pltpu.make_async_copy(ref, ref, sem).wait()

    def norm1(b):
        def chunk(i, _):
            rows = pl.ds(pl.multiple_of(i * 128, 128), 128)
            u = layer_norm(xv[b, rows, :], ln1_s[...], ln1_b[...])
            mine = pl.ds(pl.multiple_of(core * ROWS + i * 128, 128), 128)

            @pl.when(core == 0)
            def _():
                upair[b, mine, :] = u[:, :CH // 2]
                usend[b, rows, :] = u[:, CH // 2:]

            @pl.when(core == 1)
            def _():
                upair[b, mine, :] = u[:, CH // 2:]
                usend[b, rows, :] = u[:, :CH // 2]
            return 0
        lax.fori_loop(0, ROWS // 128, chunk, 0)

    def my_rows():
        return pl.ds(pl.multiple_of(core * ROWS, ROWS), ROWS)

    def send_u(b):
        remote(usend.at[b], upair.at[b, my_rows()], u_send.at[b], u_recv.at[b], partner).start()

    def hidden(b):
        arrived(usend.at[b], u_recv.at[b])

        def unit(i, _):
            cols = pl.ds(pl.multiple_of(i * 256, 256), 256)
            h = jnp.dot(w1t[...], upair[b, :, cols], preferred_element_type=F32)
            part[b, 2 * i] = h[:, :LANES]
            part[b, 2 * i + 1] = h[:, LANES:]
            return 0
        lax.fori_loop(0, 2, unit, 0)

    def blk(place, size):
        return pl.ds(pl.multiple_of(place * size, size), size)

    def scatter_start(b, p):
        src = (part, sum1, sum2)[p]
        dst = (got0, got1, got2)[p]

        def unit(q, _):
            places, strides = geometry(b, q)
            for j in range(1, RING):
                place, device = peer(places[p], strides[p], j)
                remote(src.at[b, q, blk(place, BLOCK[p])], dst.at[b, q, j - 1],
                       rs_send.at[b, p], rs_recv.at[b, p, q], device).start()
            return 0
        lax.fori_loop(0, UNITS, unit, 0)

    def scatter_add(b, p):
        src = (part, sum1, sum2)[p]
        got = (got0, got1, got2)[p]

        def unit(q, _):
            places, _ = geometry(b, q)
            arrived(got.at[b, q], rs_recv.at[b, p, q])
            total = src[b, q, blk(places[p], BLOCK[p]), :] + got[b, q, 0]
            total = total + got[b, q, 1]
            total = total + got[b, q, 2]
            if p < 2:
                (sum1, sum2)[p][b, q] = total
            else:
                base = places[0] * 128 + places[1] * 32 + places[2] * 8
                h = total + b1col[blk(base // 8, 8), :]
                g[b, core * UNITS + q, base // 8] = gelu(h).astype(BF16)
            return 0
        lax.fori_loop(0, UNITS, unit, 0)

    def owned(b, q, p, places):
        base = places[0] * 16
        if p >= 1:
            base = base + places[1] * 4
        if p >= 2:
            base = base + places[2]
        n = BLOCK[p] // 8
        return g.at[b, core * UNITS + q, blk(base // n, n)]

    def gather_start(b, p):
        def unit(q, _):
            places, strides = geometry(b, q)
            mine = owned(b, q, p, places)
            for j in range(1, RING):
                _, device = peer(places[p], strides[p], j)
                remote(mine, mine, ag_send.at[b, p], ag_recv.at[b, p, q], device).start()
            return 0
        lax.fori_loop(0, UNITS, unit, 0)

    def gather_wait(b, p):
        n = 3 * BLOCK[p] // 8

        def unit(q, _):
            arrived(g.at[b, core * UNITS + q, pl.ds(0, n)], ag_recv.at[b, p, q])
            return 0
        lax.fori_loop(0, UNITS, unit, 0)

    def swap_start(b):
        def unit(q, _):
            mine = g.at[b, core * UNITS + q]
            remote(mine, mine, d_send.at[b], d_recv.at[b, q], partner).start()
            return 0
        lax.fori_loop(0, UNITS, unit, 0)

    def swap_wait(b):
        def unit(q, _):
            arrived(g.at[b, (1 - core) * UNITS + q], d_recv.at[b, q])
            return 0
        lax.fori_loop(0, UNITS, unit, 0)

    def step(b, k):
        if k == 0:
            scatter_start(b, 0)
        elif k in (1, 2):
            scatter_add(b, k - 1)
            scatter_start(b, k)
        elif k == 3:
            scatter_add(b, 2)
            gather_start(b, 2)
        elif k in (4, 5):
            gather_wait(b, 6 - k)
            gather_start(b, 5 - k)
        elif k == 6:
            gather_wait(b, 0)
            swap_start(b)
        else:
            swap_wait(b)

    def token_mix(b):
        def pair(i, _):
            left = g[b, 2 * i].reshape(TOK, LANES)
            right = g[b, 2 * i + 1].reshape(TOK, LANES)
            t = jnp.dot(w2t[...], jnp.concatenate([left, right], axis=1), preferred_element_type=F32)
            bias = b2col[...]
            t = (t + jnp.concatenate([bias, bias], axis=1)).astype(BF16)
            cols = pl.ds(pl.multiple_of(i * 256, 256), 256)
            xv[b, :, cols] = (xv[b, :, cols].astype(F32) + t.astype(F32)).astype(BF16)
            return 0
        lax.fori_loop(0, CH // 256, pair, 0)

    def norm2(b):
        def chunk(i, _):
            rows = pl.ds(pl.multiple_of(i * 128, 128), 128)
            v[rows, :] = layer_norm(xv[b, rows, :], ln2_s[...], ln2_b[...])
            return 0
        lax.fori_loop(0, ROWS // 128, chunk, 0)

    def channel_mix(b, steps):
        acc[...] = jnp.zeros_like(acc)

        def slot(j, _):
            e = pl.ds(pl.multiple_of(j * E_TILE, E_TILE), E_TILE)
            pre = jnp.dot(v[...], wc1[:, e], preferred_element_type=F32) + b_ch1[:, e]
            act = gelu(pre).astype(BF16)
            acc[...] += jnp.dot(act, wc2[e, :], preferred_element_type=F32)
            for when, image, k in steps:
                @pl.when(j == when)
                def _():
                    step(image, k)
            return 0
        lax.fori_loop(0, N_SLOTS, slot, 0)

        def chunk(i, _):
            rows = pl.ds(pl.multiple_of(i * 64, 64), 64)
            xv[b, rows, :] = (xv[b, rows, :].astype(F32) + (acc[rows, :] + b_ch2[...])).astype(BF16)
            return 0
        lax.fori_loop(0, ROWS // 64, chunk, 0)
        pltpu.make_async_copy(xv.at[b], out_hbm.at[b], store_sem.at[b]).start()

    loads[0].wait()
    norm1(0)
    pl.semaphore_wait(barrier, 1 + 3 * (RING - 1))
    send_u(0)
    loads[1].wait()
    for i in range(4):
        rows = pl.ds(i * 256, 256)
        w1t[:, rows] = w1raw[rows, :].T
    for m in range(4):
        row = b_tok1[m:m + 1, :]
        b1col[m * LANES:(m + 1) * LANES, :] = jnp.broadcast_to(row, (LANES, LANES)).T
    hidden(0)
    step(0, 0)
    loads[2].wait()
    norm1(1)
    send_u(1)
    for m in range(4):
        row = b_tok2[pl.ds(me * 4 + m, 1), :]
        b2col[m * LANES:(m + 1) * LANES, :] = jnp.broadcast_to(row, (LANES, LANES)).T
    hidden(1)
    step(0, 1)
    step(1, 0)
    loads[3].wait()
    norm1(2)
    send_u(2)
    step(0, 2)
    loads[5].wait()
    for i in range(2):
        cols = pl.ds(i * 256, 256)
        w2t[cols, :] = w2raw[:, cols].T
    hidden(2)
    step(1, 1)
    step(0, 3)
    loads[4].wait()
    norm1(3)
    send_u(3)
    step(1, 2)
    step(0, 4)
    hidden(3)
    step(2, 0)
    step(0, 5)
    step(1, 3)
    step(0, 6)
    step(1, 4)
    step(3, 0)
    step(0, 7)
    loads[6].wait()
    loads[7].wait()

    plan = {
        0: [(0, 1, 5), (2, 2, 1), (3, 1, 6), (4, 2, 2), (5, 3, 1), (6, 2, 3), (7, 1, 7)],
        1: [(0, 3, 2), (1, 2, 4), (2, 3, 3), (3, 2, 5), (4, 3, 4), (5, 2, 6), (6, 3, 5), (7, 2, 7)],
        2: [(1, 3, 6), (5, 3, 7)],
        3: [],
    }
    for b in range(IMAGES):
        token_mix(b)
        norm2(b)
        channel_mix(b, plan[b])

    for b in range(IMAGES):
        arrived(usend.at[b], u_send.at[b])
        for p, got in enumerate((got0, got1, got2)):
            arrived(got.at[b], rs_send.at[b, p])
            arrived(g.at[b, pl.ds(0, UNITS), pl.ds(0, 3 * BLOCK[p] // 8)], ag_send.at[b, p])
        arrived(g.at[b, pl.ds(0, UNITS)], d_send.at[b])
        pltpu.make_async_copy(xv.at[b], out_hbm.at[b], store_sem.at[b]).wait()


def solution(mesh):
    row_spec = P('dp', 'sp', None)
    full_spec = P()

    def local_layer(patches, ln1_scale, ln1_bias, w_tok1, b_tok1, w_tok2, b_tok2, ln2_scale, ln2_bias, w_ch1, b_ch1, w_ch2, b_ch2):
        vmem = pl.BlockSpec(memory_space=pltpu.VMEM)
        hbm = pl.BlockSpec(memory_space=pl.ANY)
        dma = pltpu.SemaphoreType.DMA
        call = pl.pallas_call(
            layer_kernel,
            name='mixer_layer',
            out_shape=jax.ShapeDtypeStruct(patches.shape, BF16),
            in_specs=[hbm] * 5 + [vmem] * 8,
            out_specs=hbm,
            scratch_shapes=[
                pltpu.VMEM((IMAGES, ROWS, CH), BF16),
                pltpu.VMEM((2 * ROWS, TOK), BF16),
                pltpu.VMEM((TOK, ROWS), BF16),
                pltpu.VMEM((TOK, 2 * ROWS), BF16),
                pltpu.VMEM((ROWS, TOK), BF16),
                pltpu.VMEM((CH, HID), BF16),
                pltpu.VMEM((HID, CH), BF16),
                pltpu.VMEM((TOK, LANES), F32),
                pltpu.VMEM((ROWS, LANES), F32),
                pltpu.VMEM((IMAGES, ROWS, CH // 2), BF16),
                pltpu.VMEM((IMAGES, 2 * ROWS, CH // 2), BF16),
                pltpu.VMEM((IMAGES, UNITS, TOK, LANES), F32),
                pltpu.VMEM((IMAGES, UNITS, 3, BLOCK[0], LANES), F32),
                pltpu.VMEM((IMAGES, UNITS, 3, BLOCK[1], LANES), F32),
                pltpu.VMEM((IMAGES, UNITS, 3, BLOCK[2], LANES), F32),
                pltpu.VMEM((IMAGES, UNITS, BLOCK[0], LANES), F32),
                pltpu.VMEM((IMAGES, UNITS, BLOCK[1], LANES), F32),
                pltpu.VMEM((IMAGES, 2 * UNITS, TOK // 8, 8, LANES), BF16),
                pltpu.VMEM((ROWS, CH), BF16),
                pltpu.VMEM((ROWS, CH), F32),
                dma((8,)), dma((IMAGES,)),
                dma((IMAGES,)), dma((IMAGES,)),
                dma((IMAGES, 3)), dma((IMAGES, 3, UNITS)),
                dma((IMAGES, 3)), dma((IMAGES, 3, UNITS)),
                dma((IMAGES,)), dma((IMAGES, UNITS)),
            ],
            compiler_params=pltpu.CompilerParams(
                collective_id=0, has_side_effects=True, vmem_limit_bytes=64 * 1024 * 1024 - 65536),
        )
        return call(
            patches, w_tok1, w_tok2, w_ch1, w_ch2,
            ln1_scale.reshape(1, CH), ln1_bias.reshape(1, CH),
            b_tok1.reshape(TOK // LANES, LANES), b_tok2.reshape(-1, LANES),
            ln2_scale.reshape(1, CH), ln2_bias.reshape(1, CH),
            b_ch1.reshape(1, HID), b_ch2.reshape(1, CH))

    return jax.shard_map(local_layer, mesh=mesh, in_specs=(row_spec,) + (full_spec,) * 12, out_specs=row_spec, check_vma=False)
```

time: 600 us -> 114 us (0.19)
  the two profiles are of different devices: /device:TPU:5 before, /device:TPU:1 now
where the time goes in v1:
time: 114 us
  Pallas kernels  109 us (96%)
  local copies, waits for them, and re-layouts  4.64 us (4%)
    pallas_call x1, Pallas kernels, local_layer(): call(patches, w_tok1, w_tok2, w_ch1, w_ch2, ln1_scale.reshape(1, CH), ln1...  109 us
    unnamed x1, local copies, waits for them, and re-layouts  4.64 us

profile of v1, /device:TPU:1, one launch (start us, length us, event | category | flops | bytes accessed | tf_op | source)
XLA Modules:
  0.0 114.0 jit_solution(1436180159111078880)
XLA Ops:
  0.0 109.4 %mixer_layer.1 = bf16[4,512,1024]{2,1,0:T(8,128)(2,1)} custom-call(bf16[4,512,1024]{2,1,0:T(8,128)(2,1)} %x_hbm.1, bf16[65536,512]{1,0:T(8,128)(2,1)} %w_tok1_hbm.1, bf16[512,65536]{1,0:T(8,128)(2,1)} %w_tok2_hbm.1, bf16[1024,4096]{1,0:T(8,128)(2,1)} %w_ch1_hbm.1, bf16[4096,1024]{1,0:T(8,128)(2,1)} %w_ch2_hbm.1, f32[1,1024]{1,0:T(1,128)} %bitcast.10, ...), custom_call_target="tpu_custom_call" | custom-call | tf_op jit(solution)/shard_map/mixer_layer/pallas_call | solution.py:385
  109.4 4.6 %copy.15 = bf16[4,512,1024]{2,1,0:T(8,128)(2,1)} copy(bf16[4,512,1024]{2,1,0:T(8,128)(2,1)} %mixer_layer.1) | data formatting | bytes 8388608

commit v2 on v1

v2 whole, which is shorter than its diff:
```python
import functools
import math

import jax
import jax.numpy as jnp
from jax import lax
from jax.experimental import pallas as pl
from jax.experimental.pallas import tpu as pltpu
from jax.sharding import PartitionSpec as P

LN_EPS = 1e-6
IMAGES = 4
ROWS = 512
CH = 1024
TOK = 512
HID = 4096
RING = 4
DEVICES = 2 * RING ** 3
LANES = 128
UNITS = CH // 2 // LANES
BLOCK = (128, 32, 8)
NORM_ROWS = 128
ALL = (0, UNITS)
FILL = (
    (0, 1, ALL), (1, 0, (0, 2)), (0, 2, ALL), (1, 0, (2, 4)), (0, 3, ALL), (0, 4, ALL), (1, 1, ALL),
    (0, 5, ALL), (1, 2, ALL), (0, 6, ALL), (1, 3, ALL), (0, 7, ALL), (2, 0, ALL),
)
PLAN = {
    (0, 1): [(1, 4)], (0, 2): [(1, 5), (2, 1)], (0, 3): [(1, 6), (2, 2), (3, 0)],
    (1, 0): [(1, 7)], (1, 1): [(2, 3), (3, 1)], (1, 2): [(2, 4), (3, 2)], (1, 3): [(2, 5), (3, 3)],
    (2, 0): [(2, 6), (3, 4), (2, 7)], (2, 1): [(3, 5)], (2, 3): [(3, 6)],
}
F32 = jnp.float32
BF16 = jnp.bfloat16

GELU_A = math.sqrt(2.0 / math.pi)
GELU_B = GELU_A * 0.044715


def gelu(a):
    return (0.5 * a) * (1.0 + jnp.tanh(a * (GELU_A + GELU_B * (a * a))))


def layer_norm(rows, scale, offset):
    wide = rows.astype(F32)
    mean = jnp.mean(wide, axis=-1, keepdims=True)
    centered = wide - mean
    var = jnp.mean(centered * centered, axis=-1, keepdims=True)
    return (centered * lax.rsqrt(var + LN_EPS) * scale + offset).astype(BF16)


def layer_kernel(
    x_hbm, w_tok1_hbm, w_tok2_hbm, w_ch1_hbm, w_ch2_hbm,
    *rest,
):
    small, (out_hbm, *rest) = rest[:8], rest[8:]
    (
    ln1_s, ln1_b, b_tok1, b_tok2, ln2_s, ln2_b, b_ch1, b_ch2,
    xv, w1raw, w2raw, w1t, w2t, wc1, wc2, b1col, b2col,
    u, upeer, part, got0, got1, got2, sum1, sum2, g, v, acc,
    load_sem, store_sem, u_send, u_recv, rs_send, rs_recv, ag_send, ag_recv, d_send, d_recv,
    ) = rest
    me = lax.axis_index('sp')
    core = me % 2
    chip = me // 2
    partner = chip * 2 + (1 - core)

    def at(index):
        return {'sp': index}

    def geometry(b, q):
        color = (q + core + b) % 3
        places, strides = [], []
        for p in range(3):
            axis = (color + p) % 3
            stride = 1 + (3 * axis * (3 * axis - 1)) // 2
            strides.append(stride)
            places.append((chip // stride) % RING)
        return places, strides

    def peer(place, stride, j):
        other = (place + j) % RING
        return other, (chip + (other - place) * stride) * 2 + core

    loads = []

    def load(n, src, dst):
        c = pltpu.make_async_copy(src, dst, load_sem.at[n])
        c.start()
        loads.append(c)

    load(0, x_hbm.at[0], xv.at[0])
    small_vmem = (ln1_s, ln1_b, b_tok1, b_tok2, ln2_s, ln2_b, b_ch1, b_ch2)
    small_loads = [pltpu.make_async_copy(s, d, load_sem.at[8 + n]) for n, (s, d) in enumerate(zip(small, small_vmem))]
    for c in small_loads:
        c.start()
    load(1, w_tok1_hbm.at[pl.ds(pl.multiple_of(chip * (2 * ROWS), 2 * ROWS), 2 * ROWS)], w1raw)

    barrier = pltpu.get_barrier_semaphore()
    pl.semaphore_signal(barrier, inc=1, device_id=at(partner), device_id_type=pl.DeviceIdType.MESH)
    for stride in (1, 4, 16):
        place = (chip // stride) % RING
        for j in range(1, RING):
            _, other = peer(place, stride, j)
            pl.semaphore_signal(barrier, inc=1, device_id=at(other), device_id_type=pl.DeviceIdType.MESH)

    def remote(src, dst, send, recv, device):
        return pltpu.make_async_remote_copy(
            src_ref=src, dst_ref=dst, send_sem=send, recv_sem=recv,
            device_id=at(device), device_id_type=pl.DeviceIdType.MESH)

    def arrived(ref, sem):
        pltpu.make_async_copy(ref, ref, sem).wait()

    half = CH // 2
    mine = pl.ds(pl.multiple_of(core * half, half), half)
    theirs = pl.ds(pl.multiple_of((1 - core) * half, half), half)

    def norm1(b):
        for i in range(ROWS // NORM_ROWS):
            rows = pl.ds(i * NORM_ROWS, NORM_ROWS)
            u[b, rows, :] = layer_norm(xv[b, rows, :], ln1_s[...], ln1_b[...])

    def send_u(b):
        remote(u.at[b, :, theirs], upeer.at[b], u_send.at[b], u_recv.at[b], partner).start()

    def hidden(b):
        arrived(upeer.at[b], u_recv.at[b])
        own = w1t[:, pl.ds(pl.multiple_of(core * ROWS, ROWS), ROWS)]
        other = w1t[:, pl.ds(pl.multiple_of((1 - core) * ROWS, ROWS), ROWS)]
        for i in range(2):
            cols = pl.ds(pl.multiple_of(core * half + i * 256, 256), 256)
            h = (jnp.dot(own, u[b, :, cols], preferred_element_type=F32)
                 + jnp.dot(other, upeer[b, :, i * 256:(i + 1) * 256], preferred_element_type=F32))
            part[b, 2 * i] = h[:, :LANES]
            part[b, 2 * i + 1] = h[:, LANES:]
            if b == 0:
                step(0, 0, (2 * i, 2 * i + 2))

    def blk(place, size):
        return pl.ds(pl.multiple_of(place * size, size), size)

    def scatter_start(b, p, q):
        src = (part, sum1, sum2)[p]
        dst = (got0, got1, got2)[p]
        places, strides = geometry(b, q)
        for j in (2, 1, 3):
            place, device = peer(places[p], strides[p], j)
            remote(src.at[b, q, blk(place, BLOCK[p])], dst.at[b, q, j - 1],
                   rs_send.at[b, p], rs_recv.at[b, p, q], device).start()

    def scatter_add(b, p, q):
        src = (part, sum1, sum2)[p]
        got = (got0, got1, got2)[p]
        places, _ = geometry(b, q)
        arrived(got.at[b, q], rs_recv.at[b, p, q])
        total = src[b, q, blk(places[p], BLOCK[p]), :] + got[b, q, 0]
        total = total + got[b, q, 1]
        total = total + got[b, q, 2]
        if p < 2:
            (sum1, sum2)[p][b, q] = total
        else:
            base = places[0] * 128 + places[1] * 32 + places[2] * 8
            h = total + b1col[blk(base // 8, 8), :]
            g[b, core * UNITS + q, base // 8] = gelu(h).astype(BF16)

    def owned(b, q, p, places):
        base = places[0] * 16
        if p >= 1:
            base = base + places[1] * 4
        if p >= 2:
            base = base + places[2]
        n = BLOCK[p] // 8
        return g.at[b, core * UNITS + q, blk(base // n, n)]

    def gather_start(b, p, q):
        places, strides = geometry(b, q)
        piece = owned(b, q, p, places)
        for j in (2, 1, 3):
            _, device = peer(places[p], strides[p], j)
            remote(piece, piece, ag_send.at[b, p], ag_recv.at[b, p, q], device).start()

    def gather_wait(b, p, q):
        arrived(g.at[b, core * UNITS + q, pl.ds(0, 3 * BLOCK[p] // 8)], ag_recv.at[b, p, q])

    def swap_start(b, q):
        piece = g.at[b, core * UNITS + q]
        remote(piece, piece, d_send.at[b], d_recv.at[b, q], partner).start()

    def swap_wait(b, q):
        arrived(g.at[b, (1 - core) * UNITS + q], d_recv.at[b, q])

    def step(b, k, units=(0, UNITS)):
        def unit(q):
            if k == 0:
                scatter_start(b, 0, q)
            elif k in (1, 2):
                scatter_add(b, k - 1, q)
                scatter_start(b, k, q)
            elif k == 3:
                scatter_add(b, 2, q)
                gather_start(b, 2, q)
            elif k in (4, 5):
                gather_wait(b, 6 - k, q)
                gather_start(b, 5 - k, q)
            elif k == 6:
                gather_wait(b, 0, q)
                swap_start(b, q)
            else:
                swap_wait(b, q)
        with jax.named_scope(f'step_{b}_{k}'):
            for q in range(*units):
                unit(q)

    def token_mix(b):
        bias = jnp.concatenate([b2col[...], b2col[...]], axis=1)
        for i in range(CH // 256):
            left = g[b, 2 * i].reshape(TOK, LANES)
            right = g[b, 2 * i + 1].reshape(TOK, LANES)
            t = jnp.dot(w2t[...], jnp.concatenate([left, right], axis=1), preferred_element_type=F32)
            t = (t + bias).astype(BF16)
            cols = slice(i * 256, (i + 1) * 256)
            xv[b, :, cols] = (xv[b, :, cols].astype(F32) + t.astype(F32)).astype(BF16)

    def norm2(b):
        for i in range(ROWS // NORM_ROWS):
            rows = pl.ds(i * NORM_ROWS, NORM_ROWS)
            v[rows, :] = layer_norm(xv[b, rows, :], ln2_s[...], ln2_b[...])

    def mix(j, pieces):
        size = HID // pieces
        e = slice(j * size, (j + 1) * size)
        pre = jnp.dot(v[...], wc1[:, e], preferred_element_type=F32) + b_ch1[:, e]
        return jnp.dot(gelu(pre).astype(BF16), wc2[e, :], preferred_element_type=F32)

    small_loads[0].wait()
    small_loads[1].wait()
    loads[0].wait()
    load(2, x_hbm.at[1], xv.at[1])
    load(3, x_hbm.at[2], xv.at[2])
    load(4, x_hbm.at[3], xv.at[3])
    load(5, w_tok2_hbm.at[:, pl.ds(pl.multiple_of(me * ROWS, ROWS), ROWS)], w2raw)
    norm1(0)
    pl.semaphore_wait(barrier, 1 + 3 * (RING - 1))
    send_u(0)
    for c in small_loads[2:]:
        c.wait()
    loads[1].wait()
    for i in range(4):
        rows = pl.ds(i * 256, 256)
        w1t[:, rows] = w1raw[rows, :].T
    for m in range(4):
        row = b_tok1[m:m + 1, :]
        b1col[m * LANES:(m + 1) * LANES, :] = jnp.broadcast_to(row, (LANES, LANES)).T
    for m in range(4):
        row = b_tok2[pl.ds(me * 4 + m, 1), :]
        b2col[m * LANES:(m + 1) * LANES, :] = jnp.broadcast_to(row, (LANES, LANES)).T
    hidden(0)
    load(6, w_ch1_hbm, wc1)
    load(7, w_ch2_hbm, wc2)
    for b in range(1, IMAGES):
        loads[1 + b].wait()
        norm1(b)
        send_u(b)
    hidden(1)
    loads[5].wait()
    for i in range(2):
        cols = pl.ds(i * 256, 256)
        w2t[cols, :] = w2raw[:, cols].T
    hidden(2)
    hidden(3)
    for image, k, units in FILL:
        step(image, k, units)
    loads[6].wait()
    loads[7].wait()

    def point(b, r):
        for (image_at, point_at), todo in PLAN.items():
            if point_at == r:
                @pl.when(b == image_at)
                def _():
                    for image, k in todo:
                        step(image, k)

    def layer(b, _):
        point(b, 0)
        token_mix(b)
        norm2(b)
        acc[...] = mix(0, 4)
        point(b, 1)
        acc[...] += mix(1, 4)
        point(b, 2)
        acc[...] += mix(2, 4)
        point(b, 3)
        finish(b, mix(3, 4))
        return 0

    def finish(b, last):
        xv[b] = (xv[b].astype(F32) + (acc[...] + last + b_ch2[...])).astype(BF16)
        pltpu.make_async_copy(xv.at[b], out_hbm.at[b], store_sem.at[b]).start()

    lax.fori_loop(0, IMAGES - 1, layer, 0)
    b = IMAGES - 1
    step(b, 7)
    token_mix(b)
    norm2(b)
    acc[...] = mix(0, 2)
    finish(b, mix(1, 2))

    for b in range(IMAGES):
        arrived(upeer.at[b], u_send.at[b])
        for p, got in enumerate((got0, got1, got2)):
            arrived(got.at[b], rs_send.at[b, p])
            arrived(g.at[b, pl.ds(0, UNITS), pl.ds(0, 3 * BLOCK[p] // 8)], ag_send.at[b, p])
        arrived(g.at[b, pl.ds(0, UNITS)], d_send.at[b])
        pltpu.make_async_copy(xv.at[b], out_hbm.at[b], store_sem.at[b]).wait()


def solution(mesh):
    row_spec = P('dp', 'sp', None)
    full_spec = P()

    def local_layer(patches, ln1_scale, ln1_bias, w_tok1, b_tok1, w_tok2, b_tok2, ln2_scale, ln2_bias, w_ch1, b_ch1, w_ch2, b_ch2):
        hbm = pl.BlockSpec(memory_space=pl.ANY)
        dma = pltpu.SemaphoreType.DMA
        call = pl.pallas_call(
            layer_kernel,
            name='mixer_layer',
            out_shape=jax.ShapeDtypeStruct(patches.shape, BF16),
            in_specs=[hbm] * 13,
            out_specs=hbm,
            scratch_shapes=[
                *(pltpu.VMEM(s, F32) for s in ((1, CH), (1, CH), (TOK // LANES, LANES), (ROWS * DEVICES // LANES, LANES), (1, CH), (1, CH), (1, HID), (1, CH))),
                pltpu.VMEM((IMAGES, ROWS, CH), BF16),
                pltpu.VMEM((2 * ROWS, TOK), BF16),
                pltpu.VMEM((TOK, ROWS), BF16),
                pltpu.VMEM((TOK, 2 * ROWS), BF16),
                pltpu.VMEM((ROWS, TOK), BF16),
                pltpu.VMEM((CH, HID), BF16),
                pltpu.VMEM((HID, CH), BF16),
                pltpu.VMEM((TOK, LANES), F32),
                pltpu.VMEM((ROWS, LANES), F32),
                pltpu.VMEM((IMAGES, ROWS, CH), BF16),
                pltpu.VMEM((IMAGES, ROWS, CH // 2), BF16),
                pltpu.VMEM((IMAGES, UNITS, TOK, LANES), F32),
                pltpu.VMEM((IMAGES, UNITS, 3, BLOCK[0], LANES), F32),
                pltpu.VMEM((IMAGES, UNITS, 3, BLOCK[1], LANES), F32),
                pltpu.VMEM((IMAGES, UNITS, 3, BLOCK[2], LANES), F32),
                pltpu.VMEM((IMAGES, UNITS, BLOCK[0], LANES), F32),
                pltpu.VMEM((IMAGES, UNITS, BLOCK[1], LANES), F32),
                pltpu.VMEM((IMAGES, 2 * UNITS, TOK // 8, 8, LANES), BF16),
                pltpu.VMEM((ROWS, CH), BF16),
                pltpu.VMEM((ROWS, CH), F32),
                dma((16,)), dma((IMAGES,)),
                dma((IMAGES,)), dma((IMAGES,)),
                dma((IMAGES, 3)), dma((IMAGES, 3, UNITS)),
                dma((IMAGES, 3)), dma((IMAGES, 3, UNITS)),
                dma((IMAGES,)), dma((IMAGES, UNITS)),
            ],
            compiler_params=pltpu.CompilerParams(
                collective_id=0, has_side_effects=True, vmem_limit_bytes=64 * 1024 * 1024 - 65536),
        )
        return call(
            patches, w_tok1, w_tok2, w_ch1, w_ch2,
            ln1_scale.reshape(1, CH), ln1_bias.reshape(1, CH),
            b_tok1.reshape(TOK // LANES, LANES), b_tok2.reshape(-1, LANES),
            ln2_scale.reshape(1, CH), ln2_bias.reshape(1, CH),
            b_ch1.reshape(1, HID), b_ch2.reshape(1, CH))

    return jax.shard_map(local_layer, mesh=mesh, in_specs=(row_spec,) + (full_spec,) * 12, out_specs=row_spec, check_vma=False)
```

time: 114 us -> 97.5 us (0.86)
  Pallas kernels: 109 us -> 92.6 us
    pallas_call x1, Pallas kernels: 109 us -> 92.6 us  [local_layer(): call(patches, w_tok1, w_tok2, w_ch1, w_ch2, ln1_scale.reshape(1, CH), ln1...]
where the time goes in v2:
time: 97.5 us; the launch traced here: 97.3 us
  Pallas kernels  92.6 us (95%)
  local copies, waits for them, and re-layouts  4.64 us (5%)
    pallas_call x1, Pallas kernels, local_layer(): call(patches, w_tok1, w_tok2, w_ch1, w_ch2, ln1_scale.reshape(1, CH), ln1...  92.6 us
    unnamed x1, local copies, waits for them, and re-layouts  4.64 us

profile of v2, /device:TPU:1, one launch (start us, length us, event | category | flops | bytes accessed | tf_op | source)
XLA Modules:
  0.0 97.3 jit_solution(18079345103833189762)
XLA Ops:
  0.0 92.6 %mixer_layer.1 = bf16[4,512,1024]{2,1,0:T(8,128)(2,1)} custom-call(bf16[4,512,1024]{2,1,0:T(8,128)(2,1)} %x_hbm.1, bf16[65536,512]{1,0:T(8,128)(2,1)} %w_tok1_hbm.1, bf16[512,65536]{1,0:T(8,128)(2,1)} %w_tok2_hbm.1, bf16[1024,4096]{1,0:T(8,128)(2,1)} %w_ch1_hbm.1, bf16[4096,1024]{1,0:T(8,128)(2,1)} %w_ch2_hbm.1, f32[1,1024]{1,0:T(1,128)} %bitcast.10, ...), custom_call_target="tpu_custom_call" | custom-call | tf_op jit(solution)/shard_map/mixer_layer/pallas_call | solution.py:363
  92.7 4.6 %copy.15 = bf16[4,512,1024]{2,1,0:T(8,128)(2,1)} copy(bf16[4,512,1024]{2,1,0:T(8,128)(2,1)} %mixer_layer.1) | data formatting | bytes 8388608

commit v3 on v2

--- a/solution.py
+++ b/solution.py
@@ -22,13 +22,13 @@
 NORM_ROWS = 128
 ALL = (0, UNITS)
 FILL = (
-    (0, 1, ALL), (1, 0, (0, 2)), (0, 2, ALL), (1, 0, (2, 4)), (0, 3, ALL), (0, 4, ALL), (1, 1, ALL),
-    (0, 5, ALL), (1, 2, ALL), (0, 6, ALL), (1, 3, ALL), (0, 7, ALL), (2, 0, ALL),
+    (0, 1, ALL), (1, 0, (0, 2)), (0, 2, ALL), (1, 0, (2, 4)), (0, 3, ALL), (1, 1, ALL), (0, 4, ALL), (1, 2, ALL),
+    (0, 5, ALL), (1, 3, ALL), (0, 6, ALL), (2, 0, ALL), (0, 7, ALL),
 )
 PLAN = {
-    (0, 1): [(1, 4)], (0, 2): [(1, 5), (2, 1)], (0, 3): [(1, 6), (2, 2), (3, 0)],
-    (1, 0): [(1, 7)], (1, 1): [(2, 3), (3, 1)], (1, 2): [(2, 4), (3, 2)], (1, 3): [(2, 5), (3, 3)],
-    (2, 0): [(2, 6), (3, 4), (2, 7)], (2, 1): [(3, 5)], (2, 3): [(3, 6)],
+    (0, 1): [(1, 4), (2, 1)], (0, 2): [(1, 5), (2, 2)], (0, 3): [(2, 3), (1, 6), (3, 0)],
+    (1, 0): [(1, 7), (2, 4)], (1, 1): [(2, 5), (3, 1)], (1, 2): [(3, 2)], (1, 3): [(2, 6), (3, 3)],
+    (2, 0): [(2, 7), (3, 4)], (2, 1): [(3, 5)], (2, 3): [(3, 6)],
 }
 F32 = jnp.float32
 BF16 = jnp.bfloat16
@@ -305,7 +305,15 @@
     token_mix(b)
     norm2(b)
     acc[...] = mix(0, 2)
-    finish(b, mix(1, 2))
+    e = slice(HID // 2, HID)
+    pre = jnp.dot(v[...], wc1[:, e], preferred_element_type=F32) + b_ch1[:, e]
+    act = gelu(pre).astype(BF16)
+    for n in range(2):
+        cols = slice(n * half, (n + 1) * half)
+        last = jnp.dot(act, wc2[e, cols], preferred_element_type=F32)
+        xv[b, :, cols] = (xv[b, :, cols].astype(F32) + (acc[:, cols] + last + b_ch2[:, cols])).astype(BF16)
+        part_of = pl.ds(n * half, half)
+        pltpu.make_async_copy(xv.at[b, :, part_of], out_hbm.at[b, :, part_of], store_sem.at[b]).start()
 
     for b in range(IMAGES):
         arrived(upeer.at[b], u_send.at[b])

time: 97.5 us -> 96.7 us (level)
  no operation moved by 1% of the time
where the time goes in v3:
time: 96.7 us; the launch traced here: 96.5 us
  Pallas kernels  91.9 us (95%)
  local copies, waits for them, and re-layouts  4.64 us (5%)
    pallas_call x1, Pallas kernels, local_layer(): call(patches, w_tok1, w_tok2, w_ch1, w_ch2, ln1_scale.reshape(1, CH), ln1...  91.9 us
    unnamed x1, local copies, waits for them, and re-layouts  4.64 us

profile of v3, /device:TPU:1, one launch (start us, length us, event | category | flops | bytes accessed | tf_op | source)
XLA Modules:
  0.0 96.5 jit_solution(15128999995058336048)
XLA Ops:
  0.0 91.9 %mixer_layer.1 = bf16[4,512,1024]{2,1,0:T(8,128)(2,1)} custom-call(bf16[4,512,1024]{2,1,0:T(8,128)(2,1)} %x_hbm.1, bf16[65536,512]{1,0:T(8,128)(2,1)} %w_tok1_hbm.1, bf16[512,65536]{1,0:T(8,128)(2,1)} %w_tok2_hbm.1, bf16[1024,4096]{1,0:T(8,128)(2,1)} %w_ch1_hbm.1, bf16[4096,1024]{1,0:T(8,128)(2,1)} %w_ch2_hbm.1, f32[1,1024]{1,0:T(1,128)} %bitcast.10, ...), custom_call_target="tpu_custom_call" | custom-call | tf_op jit(solution)/shard_map/mixer_layer/pallas_call | solution.py:371
  91.9 4.6 %copy.15 = bf16[4,512,1024]{2,1,0:T(8,128)(2,1)} copy(bf16[4,512,1024]{2,1,0:T(8,128)(2,1)} %mixer_layer.1) | data formatting | bytes 8388608
